TPU v7x, 32 devices: a whole 2x2x4 slice. The times are simulated.
32 devices in a mesh: groups: 2 (over y), blk: 4 (over z), sub: 4 (over x, core).
Axes of the slice: x: 2, y: 2, z: 4, core: 2. Of those that a mesh axis runs over, the one named last changes fastest.
Arguments:
- dense_coef: float32 [256, 128, 128], P(('groups', 'blk'), 'sub'), parts along dimension 0, may hold values from -6 to 6
- sparse_coef: float32 [8, 128, 128], P(('groups', 'blk'), 'sub'), parts along dimension 0, may hold values from -0.0234375 to 0.0234375
- pattern: int32 [8], P('groups'), parts along dimension 0, may hold values from 0 to 159, as said below
Outputs:
- product_coef: float32 [256, 128, 128], P(('groups', 'blk'), 'sub'), parts along dimension 0
There are 2 independent parts, one for each index of `groups`. A program takes and returns all parts, laid end to end along the dimension named above; each array names one. Nothing has to cross between parts.
Inputs may be any that keep to these rules, and one draw needn't show every extreme that they name: `pattern`: the 4 entries are distinct.
All inputs are finite; a program needn't handle non-finite values.
Results may differ from a plain program's by a relative error of at most 0.000076.
Values sent between devices are 32-bit elements; how exact they have to be, the bound alone decides.
No kernel may reach another device: no remote copies, remote signals or barrier semaphores. Data moves between devices by JAX's collectives and lax.ppermute only.
A program may use at most 128 MiB of HBM per device.

v0:
```python
import math
import jax
import jax.numpy as jnp
from jax import lax
from jax.sharding import PartitionSpec as P

STEPS = 5
exact_setting = lax.Precision.HIGHEST


def shifted(block, axis, distance):
    devices = range(lax.axis_size(axis))
    route = [((i - distance) % len(devices), i) for i in devices]
    return lax.ppermute(block, axis, route)


def angle_table(row_total, col_total, period, row_start, col_start):
    row_ids = jnp.arange(row_total, dtype=jnp.int32)[:, None] + row_start
    col_ids = jnp.arange(col_total, dtype=jnp.int32)[None, :] + col_start
    phases = jnp.mod(row_ids * col_ids, period).astype(jnp.float32) * (2.0 * math.pi / period)
    return (jnp.cos(phases), jnp.sin(phases))


def forward(series_coefficients):
    col_local = series_coefficients.shape[1]
    row_total = series_coefficients.shape[2]
    padded = 2 * row_total
    col_total = col_local * lax.axis_size("sub")
    period = padded * col_total
    cosine_lookup, sine_lookup = angle_table(row_total, padded, padded, 0, 0)
    initial_real = jnp.einsum(
        "ufz,ze->ufe", series_coefficients, cosine_lookup, precision=exact_setting
    )
    initial_imaginary = -jnp.einsum(
        "ufz,ze->ufe", series_coefficients, sine_lookup, precision=exact_setting
    )
    twist_cos, twist_sin = angle_table(
        col_local, padded, period, lax.axis_index("sub") * col_local, 0
    )
    turned_real = initial_real * twist_cos + initial_imaginary * twist_sin
    turned_imag = initial_imaginary * twist_cos - initial_real * twist_sin
    stacked = jnp.stack([turned_real, turned_imag], axis=0)
    outer_cosine, outer_sine = angle_table(col_total, col_total, col_total, 0, 0)
    halves = lax.all_to_all(stacked, "sub", split_axis=3, concat_axis=2, tiled=True)
    partial_real = halves[0]
    partial_imaginary = halves[1]
    output_real = jnp.einsum(
        "rxs,xl->rsl", partial_real, outer_cosine, precision=exact_setting
    ) + jnp.einsum("rxs,xl->rsl", partial_imaginary, outer_sine, precision=exact_setting)
    output_imaginary = jnp.einsum(
        "rxs,xl->rsl", partial_imaginary, outer_cosine, precision=exact_setting
    ) - jnp.einsum("rxs,xl->rsl", partial_real, outer_sine, precision=exact_setting)
    return jnp.stack([output_real, output_imaginary], axis=0)


def flatten(halves):
    return (halves[0].reshape(halves[0].shape[0], -1), halves[1].reshape(halves[1].shape[0], -1))


def accumulate(totals, source, sparse, pattern, start):
    source_len = source[0].shape[0]
    targets = jnp.arange(totals[0].shape[0], dtype=jnp.int32)

    def one_entry(entry, running):
        wanted = start + targets - pattern[entry]
        valid = jnp.logical_and(wanted >= 0, wanted < source_len)[:, None]
        safe = jnp.clip(wanted, 0, source_len - 1)
        src_real = jnp.where(valid, jnp.take(source[0], safe, axis=0), 0.0)
        src_imag = jnp.where(valid, jnp.take(source[1], safe, axis=0), 0.0)
        sp_real = sparse[0][entry][None, :]
        sp_imag = sparse[1][entry][None, :]
        return (
            running[0] + src_real * sp_real - src_imag * sp_imag,
            running[1] + src_real * sp_imag + src_imag * sp_real,
        )

    return lax.fori_loop(0, pattern.shape[0], one_entry, totals)


def inverse(totals, local_rows, col_total):
    block_count = totals[0].shape[0]
    spectrum_real = totals[0].reshape(block_count, local_rows, col_total)
    spectrum_imaginary = totals[1].reshape(block_count, local_rows, col_total)
    padded = local_rows * lax.axis_size("sub")
    period = padded * col_total
    outer_cosine, outer_sine = angle_table(col_total, col_total, col_total, 0, 0)
    combined_real = jnp.einsum(
        "ahz,zr->arh", spectrum_real, outer_cosine, precision=exact_setting
    ) - jnp.einsum("ahz,zr->arh", spectrum_imaginary, outer_sine, precision=exact_setting)
    combined_imaginary = jnp.einsum(
        "ahz,zr->arh", spectrum_real, outer_sine, precision=exact_setting
    ) + jnp.einsum("ahz,zr->arh", spectrum_imaginary, outer_cosine, precision=exact_setting)
    twist_cos, twist_sin = angle_table(
        col_total, local_rows, period, 0, lax.axis_index("sub") * local_rows
    )
    turned_real = combined_real * twist_cos - combined_imaginary * twist_sin
    turned_imag = combined_real * twist_sin + combined_imaginary * twist_cos
    inverse_step_real, inverse_step_imaginary = (
        lax.all_to_all(turned_real, "sub", split_axis=1, concat_axis=2, tiled=True),
        lax.all_to_all(turned_imag, "sub", split_axis=1, concat_axis=2, tiled=True),
    )
    closing_cosine, closing_sine = angle_table(padded, padded, padded, 0, 0)
    value_entries = jnp.einsum(
        "xmj,jo->xmo", inverse_step_real, closing_cosine, precision=exact_setting
    ) - jnp.einsum("xmj,jo->xmo", inverse_step_imaginary, closing_sine, precision=exact_setting)
    return value_entries / period


def local(dense_coef, sparse_coef, pattern):
    block_count = dense_coef.shape[0]
    row_total = dense_coef.shape[2]
    spectra = forward(dense_coef)
    spec_shape = spectra[0].shape
    sparse = flatten(lax.all_gather(forward(sparse_coef), "blk", axis=1, tiled=True))
    empty_sum = jnp.zeros((block_count, spec_shape[1] * spec_shape[2]), jnp.float32)
    totals = (empty_sum, empty_sum)
    current = spectra
    for turn_index in range(STEPS + 1):
        if turn_index > 0:
            current = shifted(current, "blk", 1)
        totals = accumulate(totals, flatten(current), sparse, pattern, turn_index * block_count)
    value_entries = inverse(totals, spec_shape[1], spec_shape[2])
    lower_half = value_entries[:, :, :row_total]
    upper_half = value_entries[:, :, row_total:]
    carried_in = shifted(upper_half[-1:], "blk", 1)
    return lower_half + jnp.concatenate([carried_in, upper_half[:-1]], axis=0)


def solution(mesh):
    return jax.shard_map(
        local,
        mesh=mesh,
        in_specs=(
            P(("groups", "blk"), "sub", None),
            P(("groups", "blk"), "sub", None),
            P("groups"),
        ),
        out_specs=P(("groups", "blk"), "sub", None),
        check_vma=False,
    )
```

profile of v0, /device:TPU:0, one launch (start us, length us, event | category | flops | bytes accessed | tf_op | source)
XLA Modules:
  0.0 462.6 jit_solution(10227931367806987062)
XLA Ops:
  6.1 4.2 all-to-all-start.1
  14.5 7.6 %copy.18 = f32[2,32,32,256]{2,1,0,3:T(8,128)} copy(f32[2,32,32,256]{3,2,1,0:T(8,128)S(1)} %pad_maximum_fusion) | data formatting | bytes 4194304 | tf_op jit(solution)/shard_map/stack | solution.py:42
  22.1 7.1 %reshape.364 = f32[4,1,131072]{2,1,0:T(1,128)} reshape(f32[256,2,32,32]{3,2,1,0:T(8,128)} %bitcast.225) | data formatting | bytes 4194304
  29.2 4.5 all-to-all-start
  36.8 14.9 %all_gather.3 = f32[2,4,64,128]{3,2,1,0:T(8,128)S(1)} all-gather(f32[2,1,64,128]{3,2,1,0:T(8,128)S(1)} %pad_maximum_fusion.3), channel_id=1, replica_groups=mesh['groups'=2,'blk'=4,'sub'=4] {'blk'}, dimensions={1}, use_global_device_ids=true | all-gather | bytes 327680 | tf_op jit(solution)/shard_map/all_gather | solution.py:114
  52.0 7.4 %all-to-all-done = f32[4,1,131072]{2,1,0:T(1,128)} async-done(((f32[4,1,131072]{2,1,0:T(1,128)}), f32[4,1,131072]{2,1,0:T(1,128)}, u32[]{:S(2)}, u32[]{:S(2)}) %all-to-all-start) | async-done | bytes 2097184 | tf_op jit(solution)/shard_map/all_to_all | solution.py:44
  59.4 7.7 %reduce = f32[4,131072]{1,0:T(4,128)S(1)} reduce(f32[4,1,131072]{2,1,0:T(1,128)} %all-to-all-done, f32[]{:T(128)} %broadcast.711), dimensions={1}, to_apply=%all_to_all.48.reduce_sub_computation | reduce | bytes 4194308 | tf_op jit(solution)/shard_map/all_to_all | solution.py:44
  67.1 6.2 %reshape.365 = f32[256,2,32,32]{3,2,1,0:T(8,128)} reshape(f32[4,131072]{1,0:T(4,128)S(1)} %reduce) | data formatting | bytes 4194304
  73.3 8.1 %copy.19 = f32[2,32,32,4,64]{4,2,3,1,0:T(8,128)} copy(f32[2,32,32,4,64]{2,1,0,4,3:T(8,128)} %bitcast.226) | data formatting | bytes 4194304 | tf_op jit(solution)/shard_map/all_to_all | solution.py:44
  91.1 3.5 convolution_add_fusion.1
  94.6 3.9 convolution_subtract_fusion.1
  103.3 36.4 %while.101 = (s32[]{:T(128)}, f32[32,8192]{1,0:T(8,128)S(1)}, f32[32,8192]{1,0:T(8,128)}, s32[4]{0:T(128)S(1)}, f32[32,8192]{1,0:T(8,128)S(1)}, /*index=5*/f32[4...) while((s32[]{:T(128)}, f32[32,8192]{1,0:T(8,128)S(1)}, ...), condition=%wide.region_1.3_spmd.clone, body=%wide.region_0.2_spmd.clone.sunk | while | flops 3671555 | bytes 10687239 | solution.py:77
  139.7 10.1 %collective-permute-done = f32[2,32,64,128]{3,2,1,0:T(8,128)} collective-permute-done((f32[2,32,64,128]{3,2,1,0:T(8,128)}, f32[2,32,64,128]{3,2,1,0:T(8,128)}, u32[]{:S(2)}, u32[]{:S(2)}) %collective-permute-start) | collective-permute-done | bytes 2097184 | tf_op jit(solution)/shard_map/ppermute | solution.py:14
  152.7 38.5 %while.96 = (s32[]{:T(128)}, f32[32,8192]{1,0:T(8,128)S(1)}, f32[32,8192]{1,0:T(8,128)}, s32[4]{0:T(128)S(1)}, f32[32,8192]{1,0:T(8,128)S(1)}, /*index=5*/f32[4,...) while((s32[]{:T(128)}, f32[32,8192]{1,0:T(8,128)S(1)}, ...), condition=%wide.region_3.5_spmd.clone, body=%wide.region_2.4_spmd.clone.sunk | while | flops 3147330 | bytes 10687221 | solution.py:77
  158.4 4.0 multiply_add_fusion.10
  168.0 4.0 multiply_add_fusion.10
  177.7 4.0 multiply_add_fusion.10
  187.3 4.0 multiply_add_fusion.10
  191.3 10.1 %collective-permute-done.1 = f32[2,32,64,128]{3,2,1,0:T(8,128)} collective-permute-done((f32[2,32,64,128]{3,2,1,0:T(8,128)}, f32[2,32,64,128]{3,2,1,0:T(8,128)}, u32[]{:S(2)}, u32[]{:S(2)}) %collective-permute-start.1) | collective-permute-done | bytes 2097184 | tf_op jit(solution)/shard_map/ppermute | solution.py:14
  204.3 38.7 %while.97 = (s32[]{:T(128)}, f32[32,8192]{1,0:T(8,128)S(1)}, f32[32,8192]{1,0:T(8,128)}, s32[4]{0:T(128)S(1)}, f32[32,8192]{1,0:T(8,128)S(1)}, /*index=5*/f32[4,...) while((s32[]{:T(128)}, f32[32,8192]{1,0:T(8,128)S(1)}, ...), condition=%wide.region_5.7_spmd.clone, body=%wide.region_4.6_spmd.clone.sunk | while | flops 3147330 | bytes 10687221 | solution.py:77
  210.1 4.0 multiply_add_fusion.11
  219.8 4.0 multiply_add_fusion.11
  229.4 4.0 multiply_add_fusion.11
  239.0 4.0 multiply_add_fusion.11
  243.0 9.0 %collective-permute-done.2 = f32[2,32,64,128]{3,2,1,0:T(8,128)} collective-permute-done((f32[2,32,64,128]{3,2,1,0:T(8,128)}, f32[2,32,64,128]{3,2,1,0:T(8,128)}, u32[]{:S(2)}, u32[]{:S(2)}) %collective-permute-start.2) | collective-permute-done | bytes 2097184 | tf_op jit(solution)/shard_map/ppermute | solution.py:14
  255.0 38.5 %while.98 = (s32[]{:T(128)}, f32[32,8192]{1,0:T(8,128)S(1)}, f32[32,8192]{1,0:T(8,128)}, s32[4]{0:T(128)S(1)}, f32[32,8192]{1,0:T(8,128)S(1)}, /*index=5*/f32[4,...) while((s32[]{:T(128)}, f32[32,8192]{1,0:T(8,128)S(1)}, ...), condition=%wide.region_7.9_spmd.clone, body=%wide.region_6.8_spmd.clone.sunk | while | flops 3147330 | bytes 10687221 | solution.py:77
  260.7 4.0 multiply_add_fusion.12
  270.3 4.0 multiply_add_fusion.12
  279.9 4.0 multiply_add_fusion.12
  289.5 4.0 multiply_add_fusion.12
  293.5 8.4 %collective-permute-done.3 = f32[2,32,64,128]{3,2,1,0:T(8,128)} collective-permute-done((f32[2,32,64,128]{3,2,1,0:T(8,128)}, f32[2,32,64,128]{3,2,1,0:T(8,128)}, u32[]{:S(2)}, u32[]{:S(2)}) %collective-permute-start.3) | collective-permute-done | bytes 2097184 | tf_op jit(solution)/shard_map/ppermute | solution.py:14
  304.8 38.5 %while.99 = (s32[]{:T(128)}, f32[32,8192]{1,0:T(8,128)S(1)}, f32[32,8192]{1,0:T(8,128)}, s32[4]{0:T(128)S(1)}, f32[32,8192]{1,0:T(8,128)S(1)}, /*index=5*/f32[4,...) while((s32[]{:T(128)}, f32[32,8192]{1,0:T(8,128)S(1)}, ...), condition=%wide.region_9.11_spmd.clone, body=%wide.region_8.10_spmd.clone.sunk | while | flops 3147330 | bytes 10687221 | solution.py:77
  310.5 4.0 multiply_add_fusion.13
  320.1 4.0 multiply_add_fusion.13
  329.8 4.0 multiply_add_fusion.13
  339.4 4.0 multiply_add_fusion.13
  343.3 7.5 %collective-permute-done.4 = f32[2,32,64,128]{3,2,1,0:T(8,128)} collective-permute-done((f32[2,32,64,128]{3,2,1,0:T(8,128)}, f32[2,32,64,128]{3,2,1,0:T(8,128)}, u32[]{:S(2)}, u32[]{:S(2)}) %collective-permute-start.4) | collective-permute-done | bytes 2097184 | tf_op jit(solution)/shard_map/ppermute | solution.py:14
  353.7 38.7 %while.100 = (s32[]{:T(128)}, f32[32,8192]{1,0:T(8,128)S(1)}, f32[32,8192]{1,0:T(8,128)}, s32[4]{0:T(128)S(1)}, f32[32,8192]{1,0:T(8,128)S(1)}, /*index=5*/f32[4...) while((s32[]{:T(128)}, f32[32,8192]{1,0:T(8,128)S(1)}, ...), condition=%wide.region_11.13_spmd.clone, body=%wide.region_10.12_spmd.clone.sunk | while | flops 3147330 | bytes 10687221 | solution.py:77
  359.4 4.0 multiply_add_fusion.14
  369.0 4.0 multiply_add_fusion.14
  378.7 4.0 multiply_add_fusion.14
  388.3 4.0 multiply_add_fusion.14
  404.9 3.5 all-to-all-start.2
  413.9 8.9 %all-to-all-done.2 = f32[4,1,65536]{2,1,0:T(1,128)S(1)} async-done(((f32[4,1,65536]{2,1,0:T(1,128)}), f32[4,1,65536]{2,1,0:T(1,128)S(1)}, u32[]{:S(2)}, u32[]{:S(2)}) %all-to-all-start.2) | async-done | bytes 1048608 | tf_op jit(solution)/shard_map/all_to_all | solution.py:99
  423.8 4.7 %all-to-all-start.3 = ((f32[4,1,65536]{2,1,0:T(1,128)}), f32[4,1,65536]{2,1,0:T(1,128)}, u32[]{:S(2)}, u32[]{:S(2)}) async-start(f32[4,1,65536]{2,1,0:T(1,128)} %reshape.370), calls=%async_computation.3 | async-start | bytes 2097152 | tf_op jit(solution)/shard_map/all_to_all | solution.py:100
  428.5 4.6 %reduce.3 = f32[4,65536]{1,0:T(4,128)S(1)} reduce(f32[4,1,65536]{2,1,0:T(1,128)} %copy-done.4, f32[]{:T(128)} %broadcast.711), dimensions={1}, to_apply=%all_to_all.54.reduce_sub_computation | reduce | bytes 2097156 | tf_op jit(solution)/shard_map/all_to_all | solution.py:99
  443.0 4.6 %reduce.4 = f32[4,65536]{1,0:T(4,128)S(1)} reduce(f32[4,1,65536]{2,1,0:T(1,128)} %all-to-all-done.3, f32[]{:T(128)} %broadcast.711), dimensions={1}, to_apply=%all_to_all.58.reduce_sub_computation | reduce | bytes 2097156 | tf_op jit(solution)/shard_map/all_to_all | solution.py:100
  456.0 5.5 %collective-permute-done.5 = f32[1,32,128]{2,1,0:T(8,128)S(1)} collective-permute-done((f32[1,32,128]{2,1,0:T(8,128)S(1)}, f32[1,32,128]{2,1,0:T(8,128)S(1)}, u32[]{:S(2)}, u32[]{:S(2)}) %collective-permute-start.5) | collective-permute-done | bytes 16416 | tf_op jit(solution)/shard_map/ppermute | solution.py:14
  (258 shorter events, 229.5 us)
Async XLA Ops:
  0.0 10.4 %copy-start = (f32[32,32,128]{2,1,0:T(8,128)S(1)}, f32[32,32,128]{2,1,0:T(8,128)}, u32[]{:S(2)}) copy-start(f32[32,32,128]{2,1,0:T(8,128)} %param.17) | copy-start | bytes 1572868
  6.1 23.0 %all-to-all-start.1 = ((f32[4,1,4096]{2,1,0:T(1,128)}), f32[4,1,4096]{2,1,0:T(1,128)S(1)}, u32[]{:S(2)}, u32[]{:S(2)}) async-start(f32[4,1,4096]{2,1,0:T(1,128)} %reshape.366), calls=%async_computation.1 | async-start | bytes 131072 | tf_op jit(solution)/shard_map/all_to_all | solution.py:44
  29.2 30.2 %all-to-all-start = ((f32[4,1,131072]{2,1,0:T(1,128)}), f32[4,1,131072]{2,1,0:T(1,128)}, u32[]{:S(2)}, u32[]{:S(2)}) async-start(f32[4,1,131072]{2,1,0:T(1,128)} %reshape.364), calls=%async_computation | async-start | bytes 4194304 | tf_op jit(solution)/shard_map/all_to_all | solution.py:44
  100.0 49.8 %collective-permute-start = (f32[2,32,64,128]{3,2,1,0:T(8,128)}, f32[2,32,64,128]{3,2,1,0:T(8,128)}, u32[]{:S(2)}, u32[]{:S(2)}) collective-permute-start(f32[2,32,64,128]{3,2,1,0:T(8,128)} %pad_maximum_fusion.1), channel_id=1, source_target_pairs={{12,0},{0,4},{4,8},{8,12},{13,1},{1,5},{5,9},{9,13},{14,2},{2,6},{... | collective-permute-start | bytes 6291464 | tf_op jit(solution)/shard_map/ppermute | solution.py:14
  102.1 1.2 copy-start.7
  152.7 48.7 %collective-permute-start.1 = (f32[2,32,64,128]{3,2,1,0:T(8,128)}, f32[2,32,64,128]{3,2,1,0:T(8,128)}, u32[]{:S(2)}, u32[]{:S(2)}) collective-permute-start(f32[2,32,64,128]{3,2,1,0:T(8,128)} %collective-permute-done), channel_id=1, source_target_pairs={{12,0},{0,4},{4,8},{8,12},{13,1},{1,5},{5,9},{9,13},{14,2},{2,6},{... | collective-permute-start | bytes 6291464 | tf_op jit(solution)/shard_map/ppermute | solution.py:14
  204.2 47.8 %collective-permute-start.2 = (f32[2,32,64,128]{3,2,1,0:T(8,128)}, f32[2,32,64,128]{3,2,1,0:T(8,128)}, u32[]{:S(2)}, u32[]{:S(2)}) collective-permute-start(f32[2,32,64,128]{3,2,1,0:T(8,128)} %collective-permute-done.1), channel_id=1, source_target_pairs={{12,0},{0,4},{4,8},{8,12},{13,1},{1,5},{5,9},{9,13},{14,2},{2,6},{... | collective-permute-start | bytes 6291464 | tf_op jit(solution)/shard_map/ppermute | solution.py:14
  254.9 47.0 %collective-permute-start.3 = (f32[2,32,64,128]{3,2,1,0:T(8,128)}, f32[2,32,64,128]{3,2,1,0:T(8,128)}, u32[]{:S(2)}, u32[]{:S(2)}) collective-permute-start(f32[2,32,64,128]{3,2,1,0:T(8,128)} %collective-permute-done.2), channel_id=1, source_target_pairs={{12,0},{0,4},{4,8},{8,12},{13,1},{1,5},{5,9},{9,13},{14,2},{2,6},{... | collective-permute-start | bytes 6291464 | tf_op jit(solution)/shard_map/ppermute | solution.py:14
  304.7 46.1 %collective-permute-start.4 = (f32[2,32,64,128]{3,2,1,0:T(8,128)}, f32[2,32,64,128]{3,2,1,0:T(8,128)}, u32[]{:S(2)}, u32[]{:S(2)}) collective-permute-start(f32[2,32,64,128]{3,2,1,0:T(8,128)} %collective-permute-done.3), channel_id=1, source_target_pairs={{12,0},{0,4},{4,8},{8,12},{13,1},{1,5},{5,9},{9,13},{14,2},{2,6},{... | collective-permute-start | bytes 6291464 | tf_op jit(solution)/shard_map/ppermute | solution.py:14
  392.6 2.5 copy-start.2
  395.4 1.3 copy-start.5
  395.4 1.3 copy-start.6
  404.9 17.9 %all-to-all-start.2 = ((f32[4,1,65536]{2,1,0:T(1,128)}), f32[4,1,65536]{2,1,0:T(1,128)S(1)}, u32[]{:S(2)}, u32[]{:S(2)}) async-start(f32[4,1,65536]{2,1,0:T(1,128)} %reshape.368), calls=%async_computation.2 | async-start | bytes 2097152 | tf_op jit(solution)/shard_map/all_to_all | solution.py:99
  422.8 1.0 copy-start.4
  423.8 19.1 %all-to-all-start.3 = ((f32[4,1,65536]{2,1,0:T(1,128)}), f32[4,1,65536]{2,1,0:T(1,128)}, u32[]{:S(2)}, u32[]{:S(2)}) async-start(f32[4,1,65536]{2,1,0:T(1,128)} %reshape.370), calls=%async_computation.3 | async-start | bytes 2097152 | tf_op jit(solution)/shard_map/all_to_all | solution.py:100
  451.3 2.6 copy-start.3
  451.3 11.1 %copy-start.1 = (f32[32,32,128]{2,1,0:T(8,128)S(1)}, f32[32,32,128]{2,1,0:T(8,128)}, u32[]{:S(2)}) copy-start(f32[32,32,128]{2,1,0:T(8,128)} %param.17) | copy-start | bytes 1572868
  455.9 5.6 %collective-permute-start.5 = (f32[1,32,128]{2,1,0:T(8,128)S(1)}, f32[1,32,128]{2,1,0:T(8,128)S(1)}, u32[]{:S(2)}, u32[]{:S(2)}) collective-permute-start(f32[1,32,128]{2,1,0:T(8,128)S(1)} %slice.124), channel_id=1, source_target_pairs={{12,0},{0,4},{4,8},{8,12},{13,1},{1,5},{5,9},{9,13},{14,2},{2,6},{... | collective-permute-start | bytes 49160 | tf_op jit(solution)/shard_map/ppermute | solution.py:14
where the time goes:
time: 472 us; the launch traced here: 463 us
  local copies, waits for them, and re-layouts  179 us (38%)
  other arithmetic  147 us (31%)
  waiting for transfers between devices  67.4 us (14%)
  matrix products  33.5 us (7%)
  starting transfers between devices  19.3 us (4%)
  blocking collectives  14.9 us (3%)
    add x24, other arithmetic, one_entry(): running[1] + src_real * sp_imag + src_imag * sp_real  92.9 us
    ppermute x6, waiting for transfers between devices, shifted(): return lax.ppermute(block, axis, route)  50.6 us
    gather x24, local copies, waits for them, and re-layouts, one_entry(): src_real = jnp.where(valid, jnp.take(source[0], safe, axis=0), 0.0)  44.2 us
    gather x24, local copies, waits for them, and re-layouts, one_entry(): src_imag = jnp.where(valid, jnp.take(source[1], safe, axis=0), 0.0)  44 us
    unnamed x27, local copies, waits for them, and re-layouts  22.9 us
    and x24, other arithmetic, one_entry(): src_real = jnp.where(valid, jnp.take(source[0], safe, axis=0), 0.0)  15.8 us
    select_n x24, other arithmetic, one_entry(): src_real = jnp.where(valid, jnp.take(source[0], safe, axis=0), 0.0)  15.6 us
    all_gather x1, blocking collectives, local(): lax.all_gather(forward(sparse_coef), 'blk', axis=1, tiled=True)  14.9 us
  transfers between devices with their start and end apart: 10, of which 9 were waited for; matrix products, arithmetic and copies ran while one was open for 50% of the time, Pallas kernels for 0%

commit v1 on v0

--- a/solution.py
+++ b/solution.py
@@ -41,7 +41,10 @@
     turned_imag = initial_imaginary * twist_cos - initial_real * twist_sin
     stacked = jnp.stack([turned_real, turned_imag], axis=0)
     outer_cosine, outer_sine = angle_table(col_total, col_total, col_total, 0, 0)
-    halves = lax.all_to_all(stacked, "sub", split_axis=3, concat_axis=2, tiled=True)
+    halves = jnp.concatenate(
+        lax.all_to_all(jnp.stack(jnp.split(stacked, lax.axis_size("sub"), axis=3)), "sub", 0, 0),
+        axis=2,
+    )
     partial_real = halves[0]
     partial_imaginary = halves[1]
     output_real = jnp.einsum(

time: 472 us -> 451 us (0.956)
  local copies, waits for them, and re-layouts: 179 us -> 158 us
    all_to_all x3 -> x1, local copies, waits for them, and re-layouts: 8.79 us -> 0.51 us  [forward(): lax.all_to_all(jnp.stack(jnp.split(stacked, lax.axis_size('sub'), axis=3)...]
    another operation x2 -> x1, local copies, waits for them, and re-layouts: 7.74 us -> 0.08 us  [forward(): jnp.stack(jnp.split(stacked, lax.axis_size('sub'), axis=3))]
where the time goes in v1:
time: 451 us; the launch traced here: 443 us
  local copies, waits for them, and re-layouts  158 us (35%)
  other arithmetic  147 us (33%)
  waiting for transfers between devices  68.8 us (15%)
  matrix products  32.8 us (7%)
  starting transfers between devices  19.6 us (4%)
  blocking collectives  15.2 us (3%)
    add x24, other arithmetic, one_entry(): running[1] + src_real * sp_imag + src_imag * sp_real  92.4 us
    ppermute x6, waiting for transfers between devices, shifted(): return lax.ppermute(block, axis, route)  52.3 us
    gather x24, local copies, waits for them, and re-layouts, one_entry(): src_real = jnp.where(valid, jnp.take(source[0], safe, axis=0), 0.0)  44 us
    gather x24, local copies, waits for them, and re-layouts, one_entry(): src_imag = jnp.where(valid, jnp.take(source[1], safe, axis=0), 0.0)  43.8 us
    unnamed x27, local copies, waits for them, and re-layouts  18.6 us
    all_gather x1, blocking collectives, local(): lax.all_gather(forward(sparse_coef), 'blk', axis=1, tiled=True)  15.2 us
    and x24, other arithmetic, one_entry(): src_real = jnp.where(valid, jnp.take(source[0], safe, axis=0), 0.0)  15 us
    select_n x24, other arithmetic, one_entry(): src_real = jnp.where(valid, jnp.take(source[0], safe, axis=0), 0.0)  14.9 us
  transfers between devices with their start and end apart: 10, of which 9 were waited for; matrix products, arithmetic and copies ran while one was open for 50% of the time, Pallas kernels for 0%

profile of v1, /device:TPU:0, one launch (start us, length us, event | category | flops | bytes accessed | tf_op | source)
XLA Modules:
  0.0 443.3 jit_solution(7484291468514546414)
XLA Ops:
  3.9 4.2 all-to-all-start.1
  15.6 5.5 %reshape.374 = f32[4,1,131072]{2,1,0:T(1,128)} reshape(f32[4,2,32,32,64]{4,3,2,1,0:T(8,128)} %pad_maximum_fusion) | data formatting | bytes 4194304
  21.1 4.4 %all-to-all-start = ((f32[4,1,131072]{2,1,0:T(1,128)}), f32[4,1,131072]{2,1,0:T(1,128)}, u32[]{:S(2)}, u32[]{:S(2)}) async-start(f32[4,1,131072]{2,1,0:T(1,128)} %reshape.374), calls=%async_computation | async-start | bytes 4194304 | tf_op jit(solution)/shard_map/all_to_all | solution.py:45
  28.9 15.2 %all_gather.3 = f32[2,4,64,128]{3,2,1,0:T(8,128)S(1)} all-gather(f32[2,1,64,128]{3,2,1,0:T(8,128)S(1)} %pad_maximum_fusion.5), channel_id=1, replica_groups=mesh['groups'=2,'blk'=4,'sub'=4] {'blk'}, dimensions={1}, use_global_device_ids=true | all-gather | bytes 327680 | tf_op jit(solution)/shard_map/all_gather | solution.py:117
  44.3 7.0 %all-to-all-done = f32[4,1,131072]{2,1,0:T(1,128)} async-done(((f32[4,1,131072]{2,1,0:T(1,128)}), f32[4,1,131072]{2,1,0:T(1,128)}, u32[]{:S(2)}, u32[]{:S(2)}) %all-to-all-start) | async-done | bytes 2097184 | tf_op jit(solution)/shard_map/all_to_all | solution.py:45
  51.3 7.7 %reduce = f32[4,131072]{1,0:T(4,128)S(1)} reduce(f32[4,1,131072]{2,1,0:T(1,128)} %all-to-all-done, f32[]{:T(128)} %broadcast.711), dimensions={1}, to_apply=%all_to_all.32.reduce_sub_computation | reduce | bytes 4194308 | tf_op jit(solution)/shard_map/all_to_all | solution.py:45
  59.0 4.0 reshape.375
  66.2 3.5 fusion.65
  69.9 3.6 fusion.67
  73.6 3.5 convolution_subtract_fusion.1
  77.1 3.5 convolution_add_fusion.1
  85.6 35.7 %while.101 = (s32[]{:T(128)}, f32[32,8192]{1,0:T(8,128)S(1)}, f32[32,8192]{1,0:T(8,128)}, s32[4]{0:T(128)S(1)}, f32[32,8192]{1,0:T(8,128)S(1)}, /*index=5*/f32[4...) while((s32[]{:T(128)}, f32[32,8192]{1,0:T(8,128)S(1)}, ...), condition=%wide.region_1.3_spmd.clone, body=%wide.region_0.2_spmd.clone.sunk | while | flops 3671555 | bytes 10687247 | solution.py:80
  121.2 10.8 %collective-permute-done = f32[2,32,64,128]{3,2,1,0:T(8,128)} collective-permute-done((f32[2,32,64,128]{3,2,1,0:T(8,128)}, f32[2,32,64,128]{3,2,1,0:T(8,128)}, u32[]{:S(2)}, u32[]{:S(2)}) %collective-permute-start) | collective-permute-done | bytes 2097184 | tf_op jit(solution)/shard_map/ppermute | solution.py:14
  135.0 38.3 %while.96 = (s32[]{:T(128)}, f32[32,8192]{1,0:T(8,128)S(1)}, f32[32,8192]{1,0:T(8,128)}, s32[4]{0:T(128)S(1)}, f32[32,8192]{1,0:T(8,128)S(1)}, /*index=5*/f32[4,...) while((s32[]{:T(128)}, f32[32,8192]{1,0:T(8,128)S(1)}, ...), condition=%wide.region_3.5_spmd.clone, body=%wide.region_2.4_spmd.clone.sunk | while | flops 3147330 | bytes 10687229 | solution.py:80
  140.6 3.9 multiply_add_fusion.10
  150.2 3.9 multiply_add_fusion.10
  159.7 3.9 multiply_add_fusion.10
  169.3 3.9 multiply_add_fusion.10
  173.2 10.3 %collective-permute-done.1 = f32[2,32,64,128]{3,2,1,0:T(8,128)} collective-permute-done((f32[2,32,64,128]{3,2,1,0:T(8,128)}, f32[2,32,64,128]{3,2,1,0:T(8,128)}, u32[]{:S(2)}, u32[]{:S(2)}) %collective-permute-start.1) | collective-permute-done | bytes 2097184 | tf_op jit(solution)/shard_map/ppermute | solution.py:14
  186.5 37.6 %while.97 = (s32[]{:T(128)}, f32[32,8192]{1,0:T(8,128)S(1)}, f32[32,8192]{1,0:T(8,128)}, s32[4]{0:T(128)S(1)}, f32[32,8192]{1,0:T(8,128)S(1)}, /*index=5*/f32[4,...) while((s32[]{:T(128)}, f32[32,8192]{1,0:T(8,128)S(1)}, ...), condition=%wide.region_5.7_spmd.clone, body=%wide.region_4.6_spmd.clone.sunk | while | flops 3147330 | bytes 10687229 | solution.py:80
  192.0 3.9 multiply_add_fusion.11
  201.4 3.9 multiply_add_fusion.11
  210.8 3.9 multiply_add_fusion.11
  220.2 3.9 multiply_add_fusion.11
  224.2 10.1 %collective-permute-done.2 = f32[2,32,64,128]{3,2,1,0:T(8,128)} collective-permute-done((f32[2,32,64,128]{3,2,1,0:T(8,128)}, f32[2,32,64,128]{3,2,1,0:T(8,128)}, u32[]{:S(2)}, u32[]{:S(2)}) %collective-permute-start.2) | collective-permute-done | bytes 2097184 | tf_op jit(solution)/shard_map/ppermute | solution.py:14
  237.6 38.4 %while.98 = (s32[]{:T(128)}, f32[32,8192]{1,0:T(8,128)S(1)}, f32[32,8192]{1,0:T(8,128)}, s32[4]{0:T(128)S(1)}, f32[32,8192]{1,0:T(8,128)S(1)}, /*index=5*/f32[4,...) while((s32[]{:T(128)}, f32[32,8192]{1,0:T(8,128)S(1)}, ...), condition=%wide.region_7.9_spmd.clone, body=%wide.region_6.8_spmd.clone.sunk | while | flops 3147330 | bytes 10687229 | solution.py:80
  243.3 3.9 multiply_add_fusion.12
  252.9 3.9 multiply_add_fusion.12
  262.5 3.9 multiply_add_fusion.12
  272.1 3.9 multiply_add_fusion.12
  276.0 8.5 %collective-permute-done.3 = f32[2,32,64,128]{3,2,1,0:T(8,128)} collective-permute-done((f32[2,32,64,128]{3,2,1,0:T(8,128)}, f32[2,32,64,128]{3,2,1,0:T(8,128)}, u32[]{:S(2)}, u32[]{:S(2)}) %collective-permute-start.3) | collective-permute-done | bytes 2097184 | tf_op jit(solution)/shard_map/ppermute | solution.py:14
  287.5 38.9 %while.99 = (s32[]{:T(128)}, f32[32,8192]{1,0:T(8,128)S(1)}, f32[32,8192]{1,0:T(8,128)}, s32[4]{0:T(128)S(1)}, f32[32,8192]{1,0:T(8,128)S(1)}, /*index=5*/f32[4,...) while((s32[]{:T(128)}, f32[32,8192]{1,0:T(8,128)S(1)}, ...), condition=%wide.region_9.11_spmd.clone, body=%wide.region_8.10_spmd.clone.sunk | while | flops 3147330 | bytes 10687229 | solution.py:80
  293.3 3.9 multiply_add_fusion.13
  303.0 3.9 multiply_add_fusion.13
  312.7 3.9 multiply_add_fusion.13
  322.4 3.9 multiply_add_fusion.13
  326.3 7.1 %collective-permute-done.4 = f32[2,32,64,128]{3,2,1,0:T(8,128)} collective-permute-done((f32[2,32,64,128]{3,2,1,0:T(8,128)}, f32[2,32,64,128]{3,2,1,0:T(8,128)}, u32[]{:S(2)}, u32[]{:S(2)}) %collective-permute-start.4) | collective-permute-done | bytes 2097184 | tf_op jit(solution)/shard_map/ppermute | solution.py:14
  336.4 38.6 %while.100 = (s32[]{:T(128)}, f32[32,8192]{1,0:T(8,128)S(1)}, f32[32,8192]{1,0:T(8,128)}, s32[4]{0:T(128)S(1)}, f32[32,8192]{1,0:T(8,128)S(1)}, /*index=5*/f32[4...) while((s32[]{:T(128)}, f32[32,8192]{1,0:T(8,128)S(1)}, ...), condition=%wide.region_11.13_spmd.clone, body=%wide.region_10.12_spmd.clone.sunk | while | flops 3147330 | bytes 10687229 | solution.py:80
  342.0 3.9 multiply_add_fusion.14
  351.6 3.9 multiply_add_fusion.14
  361.2 3.9 multiply_add_fusion.14
  370.8 3.9 multiply_add_fusion.14
  385.8 3.5 all-to-all-start.2
  394.8 8.9 %all-to-all-done.2 = f32[4,1,65536]{2,1,0:T(1,128)S(1)} async-done(((f32[4,1,65536]{2,1,0:T(1,128)}), f32[4,1,65536]{2,1,0:T(1,128)S(1)}, u32[]{:S(2)}, u32[]{:S(2)}) %all-to-all-start.2) | async-done | bytes 1048608 | tf_op jit(solution)/shard_map/all_to_all | solution.py:102
  404.7 4.4 %all-to-all-start.3 = ((f32[4,1,65536]{2,1,0:T(1,128)}), f32[4,1,65536]{2,1,0:T(1,128)}, u32[]{:S(2)}, u32[]{:S(2)}) async-start(f32[4,1,65536]{2,1,0:T(1,128)} %reshape.380), calls=%async_computation.3 | async-start | bytes 2097152 | tf_op jit(solution)/shard_map/all_to_all | solution.py:103
  409.1 4.6 %reduce.2 = f32[4,65536]{1,0:T(4,128)S(1)} reduce(f32[4,1,65536]{2,1,0:T(1,128)} %copy-done.4, f32[]{:T(128)} %broadcast.711), dimensions={1}, to_apply=%all_to_all.34.reduce_sub_computation | reduce | bytes 2097156 | tf_op jit(solution)/shard_map/all_to_all | solution.py:102
  423.6 4.6 %reduce.3 = f32[4,65536]{1,0:T(4,128)S(1)} reduce(f32[4,1,65536]{2,1,0:T(1,128)} %all-to-all-done.3, f32[]{:T(128)} %broadcast.711), dimensions={1}, to_apply=%all_to_all.38.reduce_sub_computation | reduce | bytes 2097156 | tf_op jit(solution)/shard_map/all_to_all | solution.py:103
  436.7 5.5 %collective-permute-done.5 = f32[1,32,128]{2,1,0:T(8,128)S(1)} collective-permute-done((f32[1,32,128]{2,1,0:T(8,128)S(1)}, f32[1,32,128]{2,1,0:T(8,128)S(1)}, u32[]{:S(2)}, u32[]{:S(2)}) %collective-permute-start.5) | collective-permute-done | bytes 16416 | tf_op jit(solution)/shard_map/ppermute | solution.py:14
  (260 shorter events, 222.2 us)
Async XLA Ops:
  0.0 8.1 %copy-start = (f32[32,32,128]{2,1,0:T(8,128)S(1)}, f32[32,32,128]{2,1,0:T(8,128)}, u32[]{:S(2)}) copy-start(f32[32,32,128]{2,1,0:T(8,128)} %param.17) | copy-start | bytes 1572868
  3.9 17.3 %all-to-all-start.1 = ((f32[4,1,4096]{2,1,0:T(1,128)}), f32[4,1,4096]{2,1,0:T(1,128)S(1)}, u32[]{:S(2)}, u32[]{:S(2)}) async-start(f32[4,1,4096]{2,1,0:T(1,128)} %reshape.376), calls=%async_computation.1 | async-start | bytes 131072 | tf_op jit(solution)/shard_map/all_to_all | solution.py:45
  21.1 30.2 %all-to-all-start = ((f32[4,1,131072]{2,1,0:T(1,128)}), f32[4,1,131072]{2,1,0:T(1,128)}, u32[]{:S(2)}, u32[]{:S(2)}) async-start(f32[4,1,131072]{2,1,0:T(1,128)} %reshape.374), calls=%async_computation | async-start | bytes 4194304 | tf_op jit(solution)/shard_map/all_to_all | solution.py:45
  82.0 50.0 %collective-permute-start = (f32[2,32,64,128]{3,2,1,0:T(8,128)}, f32[2,32,64,128]{3,2,1,0:T(8,128)}, u32[]{:S(2)}, u32[]{:S(2)}) collective-permute-start(f32[2,32,64,128]{3,2,1,0:T(8,128)} %pad_maximum_fusion.1), channel_id=1, source_target_pairs={{12,0},{0,4},{4,8},{8,12},{13,1},{1,5},{5,9},{9,13},{14,2},{2,6},{... | collective-permute-start | bytes 6291464 | tf_op jit(solution)/shard_map/ppermute | solution.py:14
  84.4 1.2 copy-start.7
  134.9 48.7 %collective-permute-start.1 = (f32[2,32,64,128]{3,2,1,0:T(8,128)}, f32[2,32,64,128]{3,2,1,0:T(8,128)}, u32[]{:S(2)}, u32[]{:S(2)}) collective-permute-start(f32[2,32,64,128]{3,2,1,0:T(8,128)} %collective-permute-done), channel_id=1, source_target_pairs={{12,0},{0,4},{4,8},{8,12},{13,1},{1,5},{5,9},{9,13},{14,2},{2,6},{... | collective-permute-start | bytes 6291464 | tf_op jit(solution)/shard_map/ppermute | solution.py:14
  186.5 47.8 %collective-permute-start.2 = (f32[2,32,64,128]{3,2,1,0:T(8,128)}, f32[2,32,64,128]{3,2,1,0:T(8,128)}, u32[]{:S(2)}, u32[]{:S(2)}) collective-permute-start(f32[2,32,64,128]{3,2,1,0:T(8,128)} %collective-permute-done.1), channel_id=1, source_target_pairs={{12,0},{0,4},{4,8},{8,12},{13,1},{1,5},{5,9},{9,13},{14,2},{2,6},{... | collective-permute-start | bytes 6291464 | tf_op jit(solution)/shard_map/ppermute | solution.py:14
  237.1 47.4 %collective-permute-start.3 = (f32[2,32,64,128]{3,2,1,0:T(8,128)}, f32[2,32,64,128]{3,2,1,0:T(8,128)}, u32[]{:S(2)}, u32[]{:S(2)}) collective-permute-start(f32[2,32,64,128]{3,2,1,0:T(8,128)} %collective-permute-done.2), channel_id=1, source_target_pairs={{12,0},{0,4},{4,8},{8,12},{13,1},{1,5},{5,9},{9,13},{14,2},{2,6},{... | collective-permute-start | bytes 6291464 | tf_op jit(solution)/shard_map/ppermute | solution.py:14
  287.4 46.1 %collective-permute-start.4 = (f32[2,32,64,128]{3,2,1,0:T(8,128)}, f32[2,32,64,128]{3,2,1,0:T(8,128)}, u32[]{:S(2)}, u32[]{:S(2)}) collective-permute-start(f32[2,32,64,128]{3,2,1,0:T(8,128)} %collective-permute-done.3), channel_id=1, source_target_pairs={{12,0},{0,4},{4,8},{8,12},{13,1},{1,5},{5,9},{9,13},{14,2},{2,6},{... | collective-permute-start | bytes 6291464 | tf_op jit(solution)/shard_map/ppermute | solution.py:14
  375.1 2.5 copy-start.2
  377.8 1.3 copy-start.5
  377.9 1.3 copy-start.6
  385.8 17.9 %all-to-all-start.2 = ((f32[4,1,65536]{2,1,0:T(1,128)}), f32[4,1,65536]{2,1,0:T(1,128)S(1)}, u32[]{:S(2)}, u32[]{:S(2)}) async-start(f32[4,1,65536]{2,1,0:T(1,128)} %reshape.378), calls=%async_computation.2 | async-start | bytes 2097152 | tf_op jit(solution)/shard_map/all_to_all | solution.py:102
  403.7 1.0 copy-start.4
  404.7 18.9 %all-to-all-start.3 = ((f32[4,1,65536]{2,1,0:T(1,128)}), f32[4,1,65536]{2,1,0:T(1,128)}, u32[]{:S(2)}, u32[]{:S(2)}) async-start(f32[4,1,65536]{2,1,0:T(1,128)} %reshape.380), calls=%async_computation.3 | async-start | bytes 2097152 | tf_op jit(solution)/shard_map/all_to_all | solution.py:103
  431.9 2.6 copy-start.3
  431.9 11.1 %copy-start.1 = (f32[32,32,128]{2,1,0:T(8,128)S(1)}, f32[32,32,128]{2,1,0:T(8,128)}, u32[]{:S(2)}) copy-start(f32[32,32,128]{2,1,0:T(8,128)} %param.17) | copy-start | bytes 1572868
  436.5 5.6 %collective-permute-start.5 = (f32[1,32,128]{2,1,0:T(8,128)S(1)}, f32[1,32,128]{2,1,0:T(8,128)S(1)}, u32[]{:S(2)}, u32[]{:S(2)}) collective-permute-start(f32[1,32,128]{2,1,0:T(8,128)S(1)} %slice.124), channel_id=1, source_target_pairs={{12,0},{0,4},{4,8},{8,12},{13,1},{1,5},{5,9},{9,13},{14,2},{2,6},{... | collective-permute-start | bytes 49160 | tf_op jit(solution)/shard_map/ppermute | solution.py:14
